TPU v7x, 32 devices: a whole 2x2x4 slice. The times are simulated.
32 devices in a mesh: seq: 8 (over z, y), ch: 4 (over x, core).
Axes of the slice: x: 2, y: 2, z: 4, core: 2. Of those that a mesh axis runs over, the one named last changes fastest.
Arguments:
- signal: float32 [1, 65536, 1024], P(None, 'seq', 'ch'), may hold values from -6 to 6
- spectrum: float32 [2, 256, 256, 1024], P(None, 'seq', None, 'ch'), may hold values from -6 to 6
- channel_mode: int32 [1024], P('ch'), may hold values 0 or 1
- skip_gain: float32 [1024], P('ch'), may hold values from -4 to 4
- out_weight: bfloat16 [1024, 1024], P('ch'), may hold values from -0.1875 to 0.1875
Outputs:
- projected: float32 [1, 65536, 1024], P(None, 'seq', 'ch')
Inputs may be any that keep to these rules, and one draw needn't show every extreme that they name: `channel_mode`: 1 marks a channel whose 65536 positions are one sequence, 0 a channel whose positions form a 256 x 256 image.
All inputs are finite; a program needn't handle non-finite values. No bound on the sum of `channel_mode` on one device may be relied on, other than what follows from the above.
Results may differ from a plain program's by a relative error of at most 0.017.
Values may be sent and summed in bfloat16 or wider, within the bound.
No kernel may reach another device: no remote copies, remote signals or barrier semaphores. Data moves between devices by JAX's collectives and lax.ppermute only.
A program may use at most 192 MiB of HBM per device.

v0:
```python
import math
import jax
import jax.numpy as jnp
from jax import lax
from jax.sharding import PartitionSpec as P

ROWS = 256
COLUMNS = 256
LENGTH = 65536


def contract(pattern, operand, matrix):
    return jnp.einsum(
        pattern,
        operand,
        matrix,
        precision=lax.Precision.HIGHEST,
        preferred_element_type=jnp.float32,
    )


def phase_table(row_index, col_index, period):
    product = row_index[:, None] * col_index[None, :] % period
    angles = product.astype(jnp.float32) * (2.0 * math.pi / period)
    return (jnp.cos(angles), jnp.sin(angles))


def square_table(length):
    counter = jnp.arange(length, dtype=jnp.int32)
    return phase_table(counter, counter, length)


def transform_real(pattern, operand, cosine_table, sine_table):
    return (contract(pattern, operand, cosine_table), -contract(pattern, operand, sine_table))


def transform_complex(pattern, real_part, imag_part, cosine_table, sine_table, orient):
    real_out = contract(pattern, real_part, cosine_table) - orient * contract(
        pattern, imag_part, sine_table
    )
    imag_out = orient * contract(pattern, real_part, sine_table) + contract(
        pattern, imag_part, cosine_table
    )
    return (real_out, imag_out)


def inverse_real(pattern, real_part, imag_part, cosine_table, sine_table, factor):
    return (
        contract(pattern, real_part, cosine_table) - contract(pattern, imag_part, sine_table)
    ) * factor


def rotate(real_part, imag_part, cosine_table, sine_table, orient):
    real_out = real_part * cosine_table - orient * imag_part * sine_table
    imag_out = orient * real_part * sine_table + imag_part * cosine_table
    return (real_out, imag_out)


def filter_product(real_part, imag_part, filter_real, filter_imag):
    return (
        real_part * filter_real - imag_part * filter_imag,
        real_part * filter_imag + imag_part * filter_real,
    )


def channel_plan(signal, spectrum, channel_mode):
    groups = lax.axis_size("seq")
    position = lax.axis_index("seq")
    batches, local_len, owned = signal.shape
    rows_local = ROWS // groups
    shared = owned // groups
    tiled = signal.reshape(batches, rows_local, COLUMNS, owned)
    gathered, filters = (
        lax.all_to_all(
            tiled.astype(jnp.bfloat16), "seq", split_axis=3, concat_axis=1, tiled=True
        ).astype(tiled.dtype),
        lax.all_to_all(
            spectrum.astype(jnp.bfloat16), "seq", split_axis=3, concat_axis=1, tiled=True
        ).astype(spectrum.dtype),
    )
    own_modes = lax.dynamic_slice_in_dim(channel_mode, position * shared, shared)
    selector = (own_modes == 1)[None, :, None, None]
    images = jnp.transpose(gathered, (0, 3, 1, 2))
    filters_first = jnp.transpose(filters, (0, 3, 1, 2))
    row_cos, row_sin = square_table(ROWS)
    col_cos, col_sin = square_table(COLUMNS)
    twist_cos, twist_sin = phase_table(
        jnp.arange(ROWS, dtype=jnp.int32), jnp.arange(COLUMNS, dtype=jnp.int32), LENGTH
    )
    chosen_cos = jnp.where(selector, twist_cos[None, None], 1.0)
    chosen_sin = jnp.where(selector, twist_sin[None, None], 0.0)
    real_part, imag_part = transform_real("xmab,ad->xmdb", images, row_cos, row_sin)
    real_part, imag_part = rotate(real_part, imag_part, chosen_cos, chosen_sin, -1.0)
    real_part, imag_part = transform_complex(
        "xmdb,bc->xmdc", real_part, imag_part, col_cos, col_sin, -1.0
    )
    real_part, imag_part = filter_product(
        real_part, imag_part, filters_first[0][None], filters_first[1][None]
    )
    real_part, imag_part = transform_complex(
        "xmdc,cb->xmdb", real_part, imag_part, col_cos, col_sin, 1.0
    )
    real_part, imag_part = rotate(real_part, imag_part, chosen_cos, chosen_sin, 1.0)
    convolved = inverse_real("xmdb,da->xmab", real_part, imag_part, row_cos, row_sin, 1.0 / LENGTH)
    convolved = jnp.transpose(convolved, (0, 2, 3, 1))
    restored = lax.all_to_all(
        convolved.astype(jnp.bfloat16), "seq", split_axis=1, concat_axis=3, tiled=True
    ).astype(convolved.dtype)
    return restored.reshape(batches, local_len, owned)


def per_device(signal, spectrum, channel_mode, skip_gain, out_weight):
    convolved = channel_plan(signal, spectrum, channel_mode)
    hidden = (convolved + skip_gain[None, None, :] * signal).astype(jnp.bfloat16)
    partials = jnp.einsum("xtc,cj->xtj", hidden, out_weight, preferred_element_type=jnp.float32)
    return lax.psum_scatter(
        partials.astype(jnp.bfloat16), "ch", scatter_dimension=2, tiled=True
    ).astype(jnp.float32)


def solution(mesh):
    placed = (P(None, "seq", "ch"), P(None, "seq", None, "ch"), P("ch"), P("ch"), P("ch", None))
    return jax.shard_map(
        per_device, mesh=mesh, in_specs=placed, out_specs=P(None, "seq", "ch"), check_vma=False
    )
```

profile of v0, /device:TPU:0, one launch (start us, length us, event | category | flops | bytes accessed | tf_op | source)
XLA Modules:
  0.0 736.7 jit_solution(1022630028297481340)
XLA Ops:
  6.5 0.0 copy-start
  6.5 5.9 convert_element_type.113
  12.4 7.9 %copy.55 = bf16[1,32,256,256]{2,1,0,3:T(8,128)(2,1)} copy(bf16[1,32,256,256]{3,2,1,0:T(8,128)(2,1)} %bitcast.140) | data formatting | bytes 8388608 | tf_op jit(solution)/shard_map/convert_element_type | solution.py:75
  20.3 7.3 all-to-all-start
  27.6 16.8 %copy.62 = bf16[2,32,256,256]{2,1,0,3:T(8,128)(2,1)} copy(f32[2,32,256,256]{3,2,1,0:T(8,128)} %param.6) | data formatting | bytes 25165824 | tf_op args[1]
  44.5 0.0 copy-start.5
  44.5 76.5 %all-to-all-done = bf16[1,32,256,256]{2,1,0,3:T(8,128)(2,1)} async-done(((bf16[1,32,256,256]{2,1,0,3:T(8,128)(2,1)}), bf16[1,32,256,256]{2,1,0,3:T(8,128)(2,1)}, u32[]{:S(2)}, u32[]{:S(2)}) %all-to-all-start) | async-done | bytes 4194336 | tf_op jit(solution)/shard_map/all_to_all | solution.py:74
  120.9 5.0 all-to-all-start.1
  125.9 1.0 fusion.67
  126.9 0.1 copy.59
  127.0 1.0 fusion.68
  128.0 0.1 copy.58
  128.1 0.0 copy-done.5
  128.1 0.1 dynamic-slice_compare_fusion
  128.2 4.6 copy.56
  132.8 2.4 copy.57
  135.2 4.8 fusion.58
  140.0 0.0 copy-start.1
  140.0 5.0 fusion.50
  145.0 0.0 copy-start.2
  145.0 11.7 %fusion.55 = f32[32,256,256]{2,1,0:T(8,128)} fusion(f32[256,32,256]{2,0,1:T(8,128)S(1)} %fusion.58, f32[256,32,256]{2,0,1:T(8,128)S(1)} %fusion.50, f32[256,256]{1,0:T(8,128)S(1)} %copy.59, f32[256,256]{1,0:T(8,128)S(1)} %copy.58, pred[32]{0:T(512)(128)(4,1)S(1)} %dynamic-slice_compare_fusion), kind=kOutput, calls=%fused_computation.76 | convolution fusion | flops 6458048512 | bytes 25690144 | tf_op jit(solution)/shard_map/xmdb,bc->xmdc/dot_general | solution.py:13
  156.7 12.0 %fusion.46 = f32[32,256,256]{2,1,0:T(8,128)} fusion(f32[256,32,256]{2,0,1:T(8,128)S(1)} %fusion.58, f32[256,32,256]{2,0,1:T(8,128)S(1)} %fusion.50, f32[256,256]{1,0:T(8,128)S(1)} %copy.59, f32[256,256]{1,0:T(8,128)S(1)} %copy.58, pred[32]{0:T(512)(128)(4,1)S(1)} %dynamic-slice_compare_fusion), kind=kOutput, calls=%fused_computation.67 | convolution fusion | flops 6458048512 | bytes 25690144 | tf_op jit(solution)/shard_map/xmdb,bc->xmdc/dot_general | solution.py:13
  168.6 0.0 copy-done.1
  168.6 0.0 copy-done.2
  168.6 14.4 %multiply_subtract_fusion = f32[32,256,256]{2,1,0:T(8,128)} fusion(f32[32,256,256]{2,1,0:T(8,128)} %fusion.55, f32[256,32,256]{2,0,1:T(8,128)S(1)} %fusion.58, f32[256,32,256]{2,0,1:T(8,128)S(1)} %fusion.50, f32[256,256]{1,0:T(8,128)S(1)} %copy.59, f32[256,256]{1,0:T(8,128)S(1)} %copy.58, pred[32]{0:T(512)(128)(4,1)S(1)} %dynamic-slice_compare_fusion), kind=kOutput, calls=%fused_computation.38 | convolution fusion | flops 6462242816 | bytes 34078752 | tf_op jit(solution)/shard_map/xmdb,bc->xmdc/dot_general | solution.py:13
  183.0 125.1 %all-to-all-done.1 = bf16[2,32,256,256]{2,1,0,3:T(8,128)(2,1)} async-done(((bf16[2,32,256,256]{2,1,0,3:T(8,128)(2,1)}), bf16[2,32,256,256]{2,1,0,3:T(8,128)(2,1)}, u32[]{:S(2)}, u32[]{:S(2)}) %all-to-all-start.1) | async-done | bytes 8388640 | tf_op jit(solution)/shard_map/all_to_all | solution.py:77
  308.1 11.4 %copy.63 = bf16[2,32,256,256]{2,3,1,0:T(8,128)(2,1)} copy(bf16[2,32,256,256]{2,1,0,3:T(8,128)(2,1)} %all-to-all-done.1) | data formatting | bytes 16777216 | tf_op jit(solution)/shard_map/all_to_all | solution.py:77
  319.5 11.4 %convert_bitcast_fusion = f32[2,8,32,256,32]{3,4,1,2,0:T(8,128)} fusion(bf16[2,32,256,8,32]{2,4,3,1,0:T(8,128)(2,1)} %bitcast.138), kind=kLoop, calls=%fused_computation | loop fusion | flops 4194304 | bytes 25165824 | tf_op jit(solution)/shard_map/transpose | solution.py:84
  330.9 17.8 %copy.64 = f32[2,8,32,256,32]{3,2,1,4,0:T(8,128)} copy(f32[2,8,32,256,32]{3,4,1,2,0:T(8,128)} %convert_bitcast_fusion) | data formatting | bytes 33554432 | tf_op jit(solution)/shard_map/transpose | solution.py:84
  348.7 27.1 %fusion.19 = (f32[1,32,256,256]{3,2,1,0:T(8,128)}, f32[1,32,256,256]{3,2,1,0:T(8,128)}) fusion(f32[32,256,256]{2,1,0:T(8,128)} %multiply_subtract_fusion, f32[2,32,256,256]{3,2,1,0:T(8,128)} %bitcast.137, f32[256,32,256]{2,0,1:T(8,128)} %copy-done.1, f32[256,32,256]{2,0,1:T(8,128)} %copy-done.2, f32[256,256]{1,0:T(8,128)S(1)} %copy.59, ...), kind=kOutput, calls=%fused_computation.29 | convolution fusion | flops 6474825728 | bytes 67633184 | tf_op jit(solution)/shard_map/xmdb,bc->xmdc/dot_general | solution.py:13
  375.8 0.0 copy-start.3
  375.8 0.0 slice-start
  375.8 13.2 %fusion.14 = f32[32,256,256]{2,1,0:T(8,128)} fusion(f32[1,32,256,256]{3,2,1,0:T(8,128)} %get-tuple-element.6), kind=kOutput, calls=%fused_computation.22 | convolution fusion | flops 6443368448 | bytes 16777216 | tf_op jit(solution)/shard_map/xmdc,cb->xmdb/dot_general | solution.py:13
  389.0 0.0 copy-done.3
  389.0 0.0 slice-start.1
  389.0 11.2 %fusion.16 = f32[32,256,256]{2,1,0:T(8,128)} fusion(f32[1,32,256,256]{3,2,1,0:T(8,128)S(1)} %copy-done.3), kind=kOutput, calls=%fused_computation.24 | convolution fusion | flops 6443368448 | bytes 16777216 | tf_op jit(solution)/shard_map/xmdc,cb->xmdb/dot_general | solution.py:13
  400.1 0.0 slice-done
  400.1 0.0 slice-done.1
  400.1 10.8 %fusion.10 = f32[32,256,256]{2,1,0:T(8,128)} fusion(f32[1,32,256,256]{3,2,1,0:T(8,128)S(1)} %bitcast.134), kind=kOutput, calls=%fused_computation.18 | convolution fusion | flops 6443368448 | bytes 16777216 | tf_op jit(solution)/shard_map/xmdc,cb->xmdb/dot_general | solution.py:13
  411.0 11.0 %fusion.12 = f32[32,256,256]{2,1,0:T(8,128)} fusion(f32[1,32,256,256]{3,2,1,0:T(8,128)S(1)} %bitcast.134), kind=kOutput, calls=%fused_computation.20 | convolution fusion | flops 6443368448 | bytes 16777216 | tf_op jit(solution)/shard_map/xmdc,cb->xmdb/dot_general | solution.py:13
  422.0 19.1 %fusion.5 = f32[256,32,256]{2,0,1:T(8,128)} fusion(f32[256,256]{1,0:T(8,128)S(1)} %copy.59, f32[256,256]{1,0:T(8,128)S(1)} %copy.58, pred[32]{0:T(512)(128)(4,1)S(1)} %dynamic-slice_compare_fusion, f32[32,256,256]{2,1,0:T(8,128)} %fusion.14, f32[32,256,256]{2,1,0:T(8,128)} %fusion.10, f32[32,256,256]{2,1,0:T(8,128)} %fusion.16, f32[32,256,256]{2,1,0:T(8,128)} %fusion.12), kind=kOutput, calls=%fused_computation.15 | convolution fusion | flops 6458048512 | bytes 42467360 | tf_op jit(solution)/shard_map/xmdb,da->xmab/dot_general | solution.py:13
  441.1 20.9 %fusion.20 = bf16[1,256,256,32]{2,1,3,0:T(8,128)(2,1)} fusion(f32[256,32,256]{2,0,1:T(8,128)} %fusion.5, f32[256,256]{1,0:T(8,128)S(1)} %copy.59, f32[256,256]{1,0:T(8,128)S(1)} %copy.58, pred[32]{0:T(512)(128)(4,1)S(1)} %dynamic-slice_compare_fusion, f32[32,256,256]{2,1,0:T(8,128)} %fusion.14, f32[32,256,256]{2,1,0:T(8,128)} %fusion.10, ...), kind=kOutput, calls=%fused_computation.39 | convolution fusion | flops 6464339968 | bytes 46661664 | tf_op jit(solution)/shard_map/xmdb,da->xmab/dot_general | solution.py:13
  461.9 6.6 copy.73
  468.5 4.5 all-to-all-start.2
  473.1 0.0 reduce-scatter.2.cloned.1.call-start
  473.1 9.2 %copy.75 = f32[1,8192,256]{1,2,0:T(8,128)} copy(f32[1,8192,256]{2,1,0:T(8,128)} %param.5) | data formatting | bytes 16777216 | tf_op args[0]
  482.3 83.3 %all-to-all-done.2 = bf16[1,256,256,32]{2,3,0,1:T(8,128)(2,1)} async-done(((bf16[1,256,256,32]{2,3,0,1:T(8,128)(2,1)}), bf16[1,256,256,32]{2,3,0,1:T(8,128)(2,1)}, u32[]{:S(2)}, u32[]{:S(2)}) %all-to-all-start.2) | async-done | bytes 4194336 | tf_op jit(solution)/shard_map/all_to_all | solution.py:106
  565.6 8.0 %copy.93 = f32[1,8,32,256,32]{3,2,4,1,0:T(8,128)} copy(bf16[1,8,32,256,32]{3,4,2,1,0:T(8,128)(2,1)} %bitcast.44) | data formatting | bytes 12582912 | tf_op jit(solution)/shard_map/convert_element_type | solution.py:108
  573.6 0.0 copy-start.4
  573.6 9.4 %reshape.154 = f32[1,8192,256]{1,2,0:T(8,128)} reshape(f32[1,32,256,8,32]{2,1,4,3,0:T(8,128)} %bitcast.139) | data formatting | bytes 16777216 | tf_op jit(solution)/shard_map/convert_element_type | solution.py:108
  583.0 0.0 copy-done
  583.0 0.0 copy-done.4
  583.0 16.1 %convert_bitcast_fusion.1 = bf16[1,8192,1024]{2,1,0:T(8,128)(2,1)} fusion(bf16[256,1024]{1,0:T(8,128)(2,1)S(1)} %copy-done, f32[1,8192,256]{1,2,0:T(8,128)} %reshape.154, f32[1,8192,256]{1,2,0:T(8,128)} %copy.75, f32[256]{0:T(256)S(1)} %copy-done.4), kind=kOutput, calls=%fused_computation.1 | convolution fusion | flops 4309647360 | bytes 34079744 | tf_op jit(solution)/shard_map/xtc,cj->xtj/dot_general | solution.py:115
  599.1 0.0 reduce-scatter.2.cloned.1.call-update
  599.2 124.0 %reduce-scatter.2.cloned.1.call-done = bf16[1,8192,256]{2,1,0:T(8,128)(2,1)} async-done(((bf16[1,8192,1024]{2,1,0:T(8,128)(2,1)}), bf16[1,8192,256]{2,1,0:T(8,128)(2,1)}) %reduce-scatter.2.cloned.1.call-update) | async-done | bytes 4194320 | tf_op jit(solution)/shard_map/reduce_scatter | solution.py:116
  723.2 6.2 convert_element_type.130
  (1 shorter events, 0.0 us)
Async XLA Ops:
  6.5 576.5 %copy-start = (bf16[256,1024]{1,0:T(8,128)(2,1)S(1)}, bf16[256,1024]{1,0:T(8,128)(2,1)}, u32[]{:S(2)}) copy-start(bf16[256,1024]{1,0:T(8,128)(2,1)} %param.9) | copy-start | bytes 1572868
  20.3 100.6 %all-to-all-start = ((bf16[1,32,256,256]{2,1,0,3:T(8,128)(2,1)}), bf16[1,32,256,256]{2,1,0,3:T(8,128)(2,1)}, u32[]{:S(2)}, u32[]{:S(2)}) async-start(bf16[1,32,256,256]{2,1,0,3:T(8,128)(2,1)} %copy.55), calls=%async_computation | async-start | bytes 8388608 | tf_op jit(solution)/shard_map/all_to_all | solution.py:74
  44.5 83.6 %copy-start.5 = (s32[256]{0:T(256)S(1)}, s32[256]{0:T(256)}, u32[]{:S(2)}) copy-start(s32[256]{0:T(256)} %param.7) | copy-start | bytes 3076
  120.9 187.2 %all-to-all-start.1 = ((bf16[2,32,256,256]{2,1,0,3:T(8,128)(2,1)}), bf16[2,32,256,256]{2,1,0,3:T(8,128)(2,1)}, u32[]{:S(2)}, u32[]{:S(2)}) async-start(bf16[2,32,256,256]{2,1,0,3:T(8,128)(2,1)} %copy.62), calls=%async_computation.1 | async-start | bytes 16777216 | tf_op jit(solution)/shard_map/all_to_all | solution.py:77
  140.0 28.7 %copy-start.1 = (f32[256,32,256]{2,0,1:T(8,128)}, f32[256,32,256]{2,0,1:T(8,128)S(1)}, u32[]{:S(2)}) copy-start(f32[256,32,256]{2,0,1:T(8,128)S(1)} %fusion.58) | copy-start | bytes 25165828
  145.0 23.6 %copy-start.2 = (f32[256,32,256]{2,0,1:T(8,128)}, f32[256,32,256]{2,0,1:T(8,128)S(1)}, u32[]{:S(2)}) copy-start(f32[256,32,256]{2,0,1:T(8,128)S(1)} %fusion.50) | copy-start | bytes 25165828
  375.8 13.2 %copy-start.3 = (f32[1,32,256,256]{3,2,1,0:T(8,128)S(1)}, f32[1,32,256,256]{3,2,1,0:T(8,128)}, u32[]{:S(2)}) copy-start(f32[1,32,256,256]{3,2,1,0:T(8,128)} %get-tuple-element.6) | copy-start | bytes 25165828
  375.8 24.4 %slice-start = ((s8[8388608]{0:T(1024)(128)(4,1)}), s8[4194304]{0:T(1024)(128)(4,1)S(1)}, s32[]{:S(2)}) async-start(s8[8388608]{0:T(1024)(128)(4,1)} %bitcast.133), calls=%async_computation.5 | async-start | bytes 8388608
  389.0 11.2 %slice-start.1 = ((s8[8388608]{0:T(1024)(128)(4,1)}), s8[4194304]{0:T(1024)(128)(4,1)S(1)}, s32[]{:S(2)}) async-start(s8[8388608]{0:T(1024)(128)(4,1)} %bitcast.133), calls=%async_computation.6 | async-start | bytes 8388608
  468.5 97.0 %all-to-all-start.2 = ((bf16[1,256,256,32]{2,3,0,1:T(8,128)(2,1)}), bf16[1,256,256,32]{2,3,0,1:T(8,128)(2,1)}, u32[]{:S(2)}, u32[]{:S(2)}) async-start(bf16[1,256,256,32]{2,3,0,1:T(8,128)(2,1)} %copy.73), calls=%async_computation.2 | async-start | bytes 8388608 | tf_op jit(solution)/shard_map/all_to_all | solution.py:106
  473.1 250.1 %reduce-scatter.2.cloned.1.call-start = ((), (), s32[]{:S(2)}) async-start(), calls=%async_computation.4 | async-start | bytes 20971520 | tf_op jit(solution)/shard_map/reduce_scatter | solution.py:116
  573.6 9.4 %copy-start.4 = (f32[256]{0:T(256)S(1)}, f32[256]{0:T(256)}, u32[]{:S(2)}) copy-start(f32[256]{0:T(256)} %param.8) | copy-start | bytes 3076
Sparse Core Ops, SparseCore 0:
  599.3 123.8 reduce-scatter.1
where the time goes:
time: 748 us; the launch traced here: 737 us
  waiting for transfers between devices  409 us (55%)
  matrix products  177 us (24%)
  local copies, waits for them, and re-layouts  94.4 us (13%)
  other arithmetic  25.5 us (3%)
  starting transfers between devices  16.9 us (2%)
  between operations  14 us (2%)
    dot_general x12, matrix products, contract(): jnp.einsum(pattern, operand, matrix, precision=lax.Precision.HIGHEST, pre...  161 us
    all_to_all x1, waiting for transfers between devices, channel_plan(): lax.all_to_all(spectrum.astype(jnp.bfloat16), 'seq', split_axis=3, concat...  125 us
    reduce_scatter x1, waiting for transfers between devices, per_device(): lax.psum_scatter(partials.astype(jnp.bfloat16), 'ch', scatter_dimension=2...  124 us
    all_to_all x1, waiting for transfers between devices, channel_plan(): lax.all_to_all(convolved.astype(jnp.bfloat16), 'seq', split_axis=1, conca...  83.3 us
    all_to_all x1, waiting for transfers between devices, channel_plan(): lax.all_to_all(tiled.astype(jnp.bfloat16), 'seq', split_axis=3, concat_ax...  76.5 us
    unnamed x18, local copies, waits for them, and re-layouts  26 us
    transpose x1, local copies, waits for them, and re-layouts, channel_plan(): filters_first = jnp.transpose(filters, (0, 3, 1, 2))  17.8 us
    convert_element_type x2, local copies, waits for them, and re-layouts, channel_plan(): restored = lax.all_to_all(convolved.astype(jnp.bfloat16), 'seq', split_ax...  17.4 us
  transfers between devices with their start and end apart: 4, of which 4 were waited for; matrix products, arithmetic and copies ran while one was open for 11% of the time, Pallas kernels for 0%

commit v1 on v0

--- a/solution.py
+++ b/solution.py
@@ -71,8 +71,14 @@
     shared = owned // groups
     tiled = signal.reshape(batches, rows_local, COLUMNS, owned)
     gathered, filters = (
-        lax.all_to_all(
-            tiled.astype(jnp.bfloat16), "seq", split_axis=3, concat_axis=1, tiled=True
+        jnp.concatenate(
+            lax.all_to_all(
+                jnp.stack(jnp.split(tiled.astype(jnp.bfloat16), lax.axis_size("seq"), axis=3)),
+                "seq",
+                0,
+                0,
+            ),
+            axis=1,
         ).astype(tiled.dtype),
         lax.all_to_all(
             spectrum.astype(jnp.bfloat16), "seq", split_axis=3, concat_axis=1, tiled=True

time: 748 us -> 775 us (1.036)
  local copies, waits for them, and re-layouts: 94.4 us -> 122 us
    unnamed x18 -> x33, local copies, waits for them, and re-layouts: 26 us -> 57.4 us
    convert_element_type x1 -> x0, local copies, waits for them, and re-layouts: 7.93 us -> none  [channel_plan(): tiled.astype(jnp.bfloat16)]
  transfers between devices with their start and end apart: 4 -> 4, of which waited for: 4 -> 4; matrix products, arithmetic and copies ran while one was open for 11% -> 10% of each run, Pallas kernels for 0% -> 0%
where the time goes in v1:
time: 775 us; the launch traced here: 767 us
  waiting for transfers between devices  413 us (53%)
  matrix products  177 us (23%)
  local copies, waits for them, and re-layouts  122 us (16%)
  other arithmetic  23.5 us (3%)
  starting transfers between devices  17 us (2%)
  between operations  13.8 us (2%)
    dot_general x12, matrix products, contract(): jnp.einsum(pattern, operand, matrix, precision=lax.Precision.HIGHEST, pre...  161 us
    all_to_all x1, waiting for transfers between devices, channel_plan(): lax.all_to_all(spectrum.astype(jnp.bfloat16), 'seq', split_axis=3, concat...  130 us
    reduce_scatter x1, waiting for transfers between devices, per_device(): lax.psum_scatter(partials.astype(jnp.bfloat16), 'ch', scatter_dimension=2...  124 us
    all_to_all x1, waiting for transfers between devices, channel_plan(): lax.all_to_all(convolved.astype(jnp.bfloat16), 'seq', split_axis=1, conca...  83.2 us
    all_to_all x1, waiting for transfers between devices, channel_plan(): lax.all_to_all(jnp.stack(jnp.split(tiled.astype(jnp.bfloat16), lax.axis_s...  76.4 us
    unnamed x33, local copies, waits for them, and re-layouts  57.4 us
    transpose x1, local copies, waits for them, and re-layouts, channel_plan(): filters_first = jnp.transpose(filters, (0, 3, 1, 2))  17.8 us
    convert_element_type x2, local copies, waits for them, and re-layouts, channel_plan(): restored = lax.all_to_all(convolved.astype(jnp.bfloat16), 'seq', split_ax...  17.4 us
  transfers between devices with their start and end apart: 4, of which 4 were waited for; matrix products, arithmetic and copies ran while one was open for 10% of the time, Pallas kernels for 0%

profile of v1, /device:TPU:0, one launch (start us, length us, event | category | flops | bytes accessed | tf_op | source)
XLA Modules:
  0.0 767.3 jit_solution(16719556671051534170)
XLA Ops:
  6.5 0.0 copy-start
  6.5 3.8 convert_element_type.113
  10.4 7.2 fusion.139
  17.6 2.1 copy.89
  19.7 0.8 bitcast_dynamic-update-slice_fusion.7
  20.5 2.9 copy.90
  23.4 2.8 copy.91
  26.2 2.8 copy.92
  29.1 2.9 copy.93
  31.9 2.8 copy.94
  34.8 2.1 copy.95
  36.9 1.8 copy.96
  38.7 1.9 bitcast_dynamic-update-slice_fusion.6
  40.6 1.9 bitcast_dynamic-update-slice_fusion.5
  42.4 1.9 bitcast_dynamic-update-slice_fusion.4
  44.3 1.9 bitcast_dynamic-update-slice_fusion.3
  46.2 1.9 bitcast_dynamic-update-slice_fusion.2
  48.0 0.8 bitcast_dynamic-update-slice_fusion.1
  48.9 1.9 bitcast_dynamic-update-slice_fusion
  50.7 7.3 all-to-all-start
  58.1 16.9 %copy.58 = bf16[2,32,256,256]{2,1,0,3:T(8,128)(2,1)} copy(f32[2,32,256,256]{3,2,1,0:T(8,128)} %param.6) | data formatting | bytes 25165824 | tf_op args[1]
  74.9 76.4 %all-to-all-done = bf16[8,1,32,256,32]{3,2,4,1,0:T(8,128)(2,1)} async-done(((bf16[8,1,32,256,32]{3,2,4,1,0:T(8,128)(2,1)}), bf16[8,1,32,256,32]{3,2,4,1,0:T(8,128)(2,1)}, u32[]{:S(2)}, u32[]{:S(2)}) %all-to-all-start) | async-done | bytes 4194336 | tf_op jit(solution)/shard_map/all_to_all | solution.py:75
  151.3 5.1 all-to-all-start.1
  156.5 1.0 fusion.67
  157.5 0.1 copy.55
  157.6 1.0 fusion.68
  158.6 0.1 copy.54
  158.7 0.0 copy-done.5
  158.7 0.1 dynamic-slice_compare_fusion
  158.8 2.6 copy.53
  161.4 4.8 fusion.58
  166.2 0.0 copy-start.1
  166.2 4.8 fusion.50
  171.0 0.0 copy-start.2
  171.0 12.1 %fusion.55 = f32[32,256,256]{2,1,0:T(8,128)} fusion(f32[256,32,256]{2,0,1:T(8,128)S(1)} %fusion.58, f32[256,32,256]{2,0,1:T(8,128)S(1)} %fusion.50, f32[256,256]{1,0:T(8,128)S(1)} %copy.55, f32[256,256]{1,0:T(8,128)S(1)} %copy.54, pred[32]{0:T(512)(128)(4,1)S(1)} %dynamic-slice_compare_fusion), kind=kOutput, calls=%fused_computation.84 | convolution fusion | flops 6458048512 | bytes 25690144 | tf_op jit(solution)/shard_map/xmdb,bc->xmdc/dot_general | solution.py:13
  183.1 11.6 %fusion.46 = f32[32,256,256]{2,1,0:T(8,128)} fusion(f32[256,32,256]{2,0,1:T(8,128)S(1)} %fusion.58, f32[256,32,256]{2,0,1:T(8,128)S(1)} %fusion.50, f32[256,256]{1,0:T(8,128)S(1)} %copy.55, f32[256,256]{1,0:T(8,128)S(1)} %copy.54, pred[32]{0:T(512)(128)(4,1)S(1)} %dynamic-slice_compare_fusion), kind=kOutput, calls=%fused_computation.75 | convolution fusion | flops 6458048512 | bytes 25690144 | tf_op jit(solution)/shard_map/xmdb,bc->xmdc/dot_general | solution.py:13
  194.7 0.0 copy-done.1
  194.7 0.0 copy-done.2
  194.7 14.4 %multiply_subtract_fusion = f32[32,256,256]{2,1,0:T(8,128)} fusion(f32[32,256,256]{2,1,0:T(8,128)} %fusion.55, f32[256,32,256]{2,0,1:T(8,128)S(1)} %fusion.58, f32[256,32,256]{2,0,1:T(8,128)S(1)} %fusion.50, f32[256,256]{1,0:T(8,128)S(1)} %copy.55, f32[256,256]{1,0:T(8,128)S(1)} %copy.54, pred[32]{0:T(512)(128)(4,1)S(1)} %dynamic-slice_compare_fusion), kind=kOutput, calls=%fused_computation.38 | convolution fusion | flops 6462242816 | bytes 34078752 | tf_op jit(solution)/shard_map/xmdb,bc->xmdc/dot_general | solution.py:13
  209.1 129.6 %all-to-all-done.1 = bf16[2,32,256,256]{2,1,0,3:T(8,128)(2,1)} async-done(((bf16[2,32,256,256]{2,1,0,3:T(8,128)(2,1)}), bf16[2,32,256,256]{2,1,0,3:T(8,128)(2,1)}, u32[]{:S(2)}, u32[]{:S(2)}) %all-to-all-start.1) | async-done | bytes 8388640 | tf_op jit(solution)/shard_map/all_to_all | solution.py:83
  338.7 11.4 %copy.59 = bf16[2,32,256,256]{2,3,1,0:T(8,128)(2,1)} copy(bf16[2,32,256,256]{2,1,0,3:T(8,128)(2,1)} %all-to-all-done.1) | data formatting | bytes 16777216 | tf_op jit(solution)/shard_map/all_to_all | solution.py:83
  350.1 11.4 %convert_bitcast_fusion = f32[2,8,32,256,32]{3,4,1,2,0:T(8,128)} fusion(bf16[2,32,256,8,32]{2,4,3,1,0:T(8,128)(2,1)} %bitcast.152), kind=kLoop, calls=%fused_computation | loop fusion | flops 4194304 | bytes 25165824 | tf_op jit(solution)/shard_map/transpose | solution.py:90
  361.5 17.8 %copy.60 = f32[2,8,32,256,32]{3,2,1,4,0:T(8,128)} copy(f32[2,8,32,256,32]{3,4,1,2,0:T(8,128)} %convert_bitcast_fusion) | data formatting | bytes 33554432 | tf_op jit(solution)/shard_map/transpose | solution.py:90
  379.2 27.1 %fusion.19 = (f32[1,32,256,256]{3,2,1,0:T(8,128)}, f32[1,32,256,256]{3,2,1,0:T(8,128)}) fusion(f32[32,256,256]{2,1,0:T(8,128)} %multiply_subtract_fusion, f32[2,32,256,256]{3,2,1,0:T(8,128)} %bitcast.151, f32[256,32,256]{2,0,1:T(8,128)} %copy-done.1, f32[256,32,256]{2,0,1:T(8,128)} %copy-done.2, f32[256,256]{1,0:T(8,128)S(1)} %copy.55, ...), kind=kOutput, calls=%fused_computation.29 | convolution fusion | flops 6474825728 | bytes 67633184 | tf_op jit(solution)/shard_map/xmdb,bc->xmdc/dot_general | solution.py:13
  406.4 13.2 %fusion.14 = f32[32,256,256]{2,1,0:T(8,128)} fusion(f32[1,32,256,256]{3,2,1,0:T(8,128)} %get-tuple-element.6), kind=kOutput, calls=%fused_computation.22 | convolution fusion | flops 6443368448 | bytes 16777216 | tf_op jit(solution)/shard_map/xmdc,cb->xmdb/dot_general | solution.py:13
  419.6 0.0 copy-done.3
  419.6 11.2 %fusion.16 = f32[32,256,256]{2,1,0:T(8,128)} fusion(f32[1,32,256,256]{3,2,1,0:T(8,128)S(1)} %copy-done.3), kind=kOutput, calls=%fused_computation.24 | convolution fusion | flops 6443368448 | bytes 16777216 | tf_op jit(solution)/shard_map/xmdc,cb->xmdb/dot_general | solution.py:13
  430.8 0.0 slice-done
  430.8 0.0 slice-done.1
  430.8 10.8 %fusion.10 = f32[32,256,256]{2,1,0:T(8,128)} fusion(f32[1,32,256,256]{3,2,1,0:T(8,128)S(1)} %bitcast.148), kind=kOutput, calls=%fused_computation.18 | convolution fusion | flops 6443368448 | bytes 16777216 | tf_op jit(solution)/shard_map/xmdc,cb->xmdb/dot_general | solution.py:13
  441.7 11.0 %fusion.12 = f32[32,256,256]{2,1,0:T(8,128)} fusion(f32[1,32,256,256]{3,2,1,0:T(8,128)S(1)} %bitcast.148), kind=kOutput, calls=%fused_computation.20 | convolution fusion | flops 6443368448 | bytes 16777216 | tf_op jit(solution)/shard_map/xmdc,cb->xmdb/dot_general | solution.py:13
  452.7 19.1 %fusion.5 = f32[256,32,256]{2,0,1:T(8,128)} fusion(f32[256,256]{1,0:T(8,128)S(1)} %copy.55, f32[256,256]{1,0:T(8,128)S(1)} %copy.54, pred[32]{0:T(512)(128)(4,1)S(1)} %dynamic-slice_compare_fusion, f32[32,256,256]{2,1,0:T(8,128)} %fusion.14, f32[32,256,256]{2,1,0:T(8,128)} %fusion.10, f32[32,256,256]{2,1,0:T(8,128)} %fusion.16, f32[32,256,256]{2,1,0:T(8,128)} %fusion.12), kind=kOutput, calls=%fused_computation.15 | convolution fusion | flops 6458048512 | bytes 42467360 | tf_op jit(solution)/shard_map/xmdb,da->xmab/dot_general | solution.py:13
  471.8 20.9 %fusion.20 = bf16[1,256,256,32]{2,1,3,0:T(8,128)(2,1)} fusion(f32[256,32,256]{2,0,1:T(8,128)} %fusion.5, f32[256,256]{1,0:T(8,128)S(1)} %copy.55, f32[256,256]{1,0:T(8,128)S(1)} %copy.54, pred[32]{0:T(512)(128)(4,1)S(1)} %dynamic-slice_compare_fusion, f32[32,256,256]{2,1,0:T(8,128)} %fusion.14, f32[32,256,256]{2,1,0:T(8,128)} %fusion.10, ...), kind=kOutput, calls=%fused_computation.39 | convolution fusion | flops 6464339968 | bytes 46661664 | tf_op jit(solution)/shard_map/xmdb,da->xmab/dot_general | solution.py:13
  492.7 6.6 copy.69
  499.3 4.6 all-to-all-start.2
  503.9 0.0 reduce-scatter.2.cloned.1.call-start
  503.9 9.2 %copy.71 = f32[1,8192,256]{1,2,0:T(8,128)} copy(f32[1,8192,256]{2,1,0:T(8,128)} %param.5) | data formatting | bytes 16777216 | tf_op args[0]
  513.1 83.2 %all-to-all-done.2 = bf16[1,256,256,32]{2,3,0,1:T(8,128)(2,1)} async-done(((bf16[1,256,256,32]{2,3,0,1:T(8,128)(2,1)}), bf16[1,256,256,32]{2,3,0,1:T(8,128)(2,1)}, u32[]{:S(2)}, u32[]{:S(2)}) %all-to-all-start.2) | async-done | bytes 4194336 | tf_op jit(solution)/shard_map/all_to_all | solution.py:112
  596.3 8.0 %copy.98 = f32[1,8,32,256,32]{3,2,4,1,0:T(8,128)} copy(bf16[1,8,32,256,32]{3,4,2,1,0:T(8,128)(2,1)} %bitcast.49) | data formatting | bytes 12582912 | tf_op jit(solution)/shard_map/convert_element_type | solution.py:114
  604.4 9.4 %reshape.158 = f32[1,8192,256]{1,2,0:T(8,128)} reshape(f32[1,32,256,8,32]{2,1,4,3,0:T(8,128)} %bitcast.153) | data formatting | bytes 16777216 | tf_op jit(solution)/shard_map/convert_element_type | solution.py:114
  613.8 16.1 %convert_bitcast_fusion.1 = bf16[1,8192,1024]{2,1,0:T(8,128)(2,1)} fusion(bf16[256,1024]{1,0:T(8,128)(2,1)S(1)} %copy-done, f32[1,8192,256]{1,2,0:T(8,128)} %reshape.158, f32[1,8192,256]{1,2,0:T(8,128)} %copy.71, f32[256]{0:T(256)S(1)} %copy-done.4), kind=kOutput, calls=%fused_computation.1 | convolution fusion | flops 4309647360 | bytes 34079744 | tf_op jit(solution)/shard_map/xtc,cj->xtj/dot_general | solution.py:121
  629.9 0.0 reduce-scatter.2.cloned.1.call-update
  629.9 124.0 %reduce-scatter.2.cloned.1.call-done = bf16[1,8192,256]{2,1,0:T(8,128)(2,1)} async-done(((bf16[1,8192,1024]{2,1,0:T(8,128)(2,1)}), bf16[1,8192,256]{2,1,0:T(8,128)(2,1)}) %reduce-scatter.2.cloned.1.call-update) | async-done | bytes 4194320 | tf_op jit(solution)/shard_map/reduce_scatter | solution.py:122
  754.0 6.2 convert_element_type.130
  (8 shorter events, 0.0 us)
Async XLA Ops:
  6.5 607.2 %copy-start = (bf16[256,1024]{1,0:T(8,128)(2,1)S(1)}, bf16[256,1024]{1,0:T(8,128)(2,1)}, u32[]{:S(2)}) copy-start(bf16[256,1024]{1,0:T(8,128)(2,1)} %param.9) | copy-start | bytes 1572868
  50.7 100.6 %all-to-all-start = ((bf16[8,1,32,256,32]{3,2,4,1,0:T(8,128)(2,1)}), bf16[8,1,32,256,32]{3,2,4,1,0:T(8,128)(2,1)}, u32[]{:S(2)}, u32[]{:S(2)}) async-start(bf16[8,1,32,256,32]{3,2,4,1,0:T(8,128)(2,1)} %bitcast_dynamic-update-slice_fusion), calls=%async_computation | async-start | bytes 8388608 | tf_op jit(solution)/shard_map/all_to_all | solution.py:75
  74.9 83.8 %copy-start.5 = (s32[256]{0:T(256)S(1)}, s32[256]{0:T(256)}, u32[]{:S(2)}) copy-start(s32[256]{0:T(256)} %param.7) | copy-start | bytes 3076
  151.3 187.4 %all-to-all-start.1 = ((bf16[2,32,256,256]{2,1,0,3:T(8,128)(2,1)}), bf16[2,32,256,256]{2,1,0,3:T(8,128)(2,1)}, u32[]{:S(2)}, u32[]{:S(2)}) async-start(bf16[2,32,256,256]{2,1,0,3:T(8,128)(2,1)} %copy.58), calls=%async_computation.1 | async-start | bytes 16777216 | tf_op jit(solution)/shard_map/all_to_all | solution.py:83
  166.2 28.5 %copy-start.1 = (f32[256,32,256]{2,0,1:T(8,128)}, f32[256,32,256]{2,0,1:T(8,128)S(1)}, u32[]{:S(2)}) copy-start(f32[256,32,256]{2,0,1:T(8,128)S(1)} %fusion.58) | copy-start | bytes 25165828
  171.0 23.7 %copy-start.2 = (f32[256,32,256]{2,0,1:T(8,128)}, f32[256,32,256]{2,0,1:T(8,128)S(1)}, u32[]{:S(2)}) copy-start(f32[256,32,256]{2,0,1:T(8,128)S(1)} %fusion.50) | copy-start | bytes 25165828
  406.4 13.2 %copy-start.3 = (f32[1,32,256,256]{3,2,1,0:T(8,128)S(1)}, f32[1,32,256,256]{3,2,1,0:T(8,128)}, u32[]{:S(2)}) copy-start(f32[1,32,256,256]{3,2,1,0:T(8,128)} %get-tuple-element.6) | copy-start | bytes 25165828
  406.4 24.5 %slice-start = ((s8[8388608]{0:T(1024)(128)(4,1)}), s8[4194304]{0:T(1024)(128)(4,1)S(1)}, s32[]{:S(2)}) async-start(s8[8388608]{0:T(1024)(128)(4,1)} %bitcast.147), calls=%async_computation.5 | async-start | bytes 8388608
  419.6 11.2 %slice-start.1 = ((s8[8388608]{0:T(1024)(128)(4,1)}), s8[4194304]{0:T(1024)(128)(4,1)S(1)}, s32[]{:S(2)}) async-start(s8[8388608]{0:T(1024)(128)(4,1)} %bitcast.147), calls=%async_computation.6 | async-start | bytes 8388608
  499.3 97.0 %all-to-all-start.2 = ((bf16[1,256,256,32]{2,3,0,1:T(8,128)(2,1)}), bf16[1,256,256,32]{2,3,0,1:T(8,128)(2,1)}, u32[]{:S(2)}, u32[]{:S(2)}) async-start(bf16[1,256,256,32]{2,3,0,1:T(8,128)(2,1)} %copy.69), calls=%async_computation.2 | async-start | bytes 8388608 | tf_op jit(solution)/shard_map/all_to_all | solution.py:112
  503.9 250.1 %reduce-scatter.2.cloned.1.call-start = ((), (), s32[]{:S(2)}) async-start(), calls=%async_computation.4 | async-start | bytes 20971520 | tf_op jit(solution)/shard_map/reduce_scatter | solution.py:122
  604.4 9.4 %copy-start.4 = (f32[256]{0:T(256)S(1)}, f32[256]{0:T(256)}, u32[]{:S(2)}) copy-start(f32[256]{0:T(256)} %param.8) | copy-start | bytes 3076
Sparse Core Ops, SparseCore 0:
  630.0 123.8 reduce-scatter.1
